TPU v7x, 32 devices: a whole 2x2x4 slice. The times are simulated.
32 devices in a mesh: space: 16 (over z, y, core), tm: 2 (over x).
Axes of the slice: x: 2, y: 2, z: 4, core: 2. Of those that a mesh axis runs over, the one named last changes fastest.
Arguments:
- solutions: bfloat16 [2, 12, 8192, 128], P('tm', None, 'space'), may hold values from -6 to 6
- noise: int32 [2, 64, 12, 8192], P('tm', None, None, 'space'), may hold values from 0 to 3
- momenta: int32 [27, 3], replicated, may hold values from -2 to 2
- pairs: int32 [16, 2], P('tm'), may hold values from 0 to 1
Outputs:
- mesons: float32 [2, 2, 27, 64, 64], P('tm', None, None, 'space')
- correlators: float32 [16, 2, 27], P('tm')
All inputs are finite; a program needn't handle non-finite values.
Results may differ from a plain program's by a relative error of at most 0.002.
Values sent between devices are 32-bit elements; how exact they have to be, the bound alone decides.
A program may use at most 64 MiB of HBM per device.

v0:
```python
import math
import jax
import jax.numpy as jnp
from jax import lax
from jax.sharding import PartitionSpec as P

EXTENT = 48


def phase_weights(noise_block, momenta, coords):
    qdotx = (
        momenta[:, 0:1] * coords[0][None, :]
        + momenta[:, 1:2] * coords[1][None, :]
        + momenta[:, 2:3] * coords[2][None, :]
    )
    base_index = qdotx % EXTENT
    angle = base_index.astype(jnp.float32) * jnp.float32(2.0 * math.pi / EXTENT)
    base_re = jnp.cos(angle).astype(jnp.bfloat16)[:, None, None, :]
    base_im = (-jnp.sin(angle)).astype(jnp.bfloat16)[:, None, None, :]
    turns = (noise_block % 4)[None, :, :, :]
    weight_re = jnp.where(
        turns == 0,
        base_re,
        jnp.where(turns == 1, base_im, jnp.where(turns == 2, -base_re, -base_im)),
    )
    weight_im = jnp.where(
        turns == 0,
        base_im,
        jnp.where(turns == 1, -base_re, jnp.where(turns == 2, -base_im, base_re)),
    )
    rows = momenta.shape[0] * noise_block.shape[0]
    cols = noise_block.shape[1] * noise_block.shape[2]
    return (weight_re.reshape(rows, cols), weight_im.reshape(rows, cols))


def partial_field(vectors, sources, momenta, offset):
    spincol, sites, width = vectors.shape
    nvec = width // 2
    moms = momenta.shape[0]
    block = min(128, sites)
    nblocks = sites // block

    def one_block(step, total):
        first = (step * block).astype(jnp.int32)
        noise_block = lax.dynamic_slice_in_dim(sources, first, block, 2)
        vec_block = lax.dynamic_slice_in_dim(vectors, first, block, 1)
        glob = offset + first + jnp.arange(block, dtype=jnp.int32)
        coords = (glob % EXTENT, glob // EXTENT % EXTENT, glob // (EXTENT * EXTENT))
        weight_re, weight_im = phase_weights(noise_block, momenta, coords)
        stacked = vec_block.reshape(spincol * block, width)
        left = jnp.dot(weight_re, stacked, preferred_element_type=jnp.float32)
        right = jnp.dot(weight_im, stacked, preferred_element_type=jnp.float32)
        real_part = left[:, :nvec] - right[:, nvec:]
        imag_part = left[:, nvec:] + right[:, :nvec]
        return total + jnp.stack([real_part, imag_part], 0)

    start = jnp.zeros((2, moms * nvec, nvec), jnp.float32)
    total = lax.fori_loop(0, nblocks, one_block, start)
    return total.reshape(2, moms, nvec, nvec)


def pair_traces(fields, pairs):
    nslices = fields.shape[0]
    slots = jnp.arange(nslices, dtype=jnp.int32)
    pick_sink = (pairs[:, 1][:, None] == slots[None, :]).astype(jnp.float32)
    pick_source = (pairs[:, 0][:, None] == slots[None, :]).astype(jnp.float32)
    sink = jnp.einsum("kt,tcpij->kcpij", pick_sink, fields, precision=lax.Precision.HIGHEST)
    source = jnp.einsum("kt,tcpij->kcpij", pick_source, fields, precision=lax.Precision.HIGHEST)
    real_part = jnp.sum(sink[:, 0] * source[:, 0] + sink[:, 1] * source[:, 1], axis=(2, 3))
    imag_part = jnp.sum(sink[:, 1] * source[:, 0] - sink[:, 0] * source[:, 1], axis=(2, 3))
    return jnp.stack([real_part, imag_part], 1)


def local(solutions, noise, momenta, pairs):
    slice_count, spincol, sites_local, width = solutions.shape
    nvec = width // 2
    nspace = lax.axis_size("space")
    scale = 1.0 / math.sqrt(spincol * sites_local * nspace)
    offset = lax.axis_index("space") * sites_local
    terms = jnp.stack([partial_field(solutions[0], noise[0], momenta, offset) * scale], 0)
    mesons = lax.psum_scatter(terms, "space", scatter_dimension=3, tiled=True)
    every_slice = lax.all_gather(mesons, "tm", axis=0, tiled=True)
    partial_traces = pair_traces(every_slice, pairs)
    correlators = lax.psum(partial_traces, "space") / nvec
    return (mesons, correlators)


def solution(mesh):
    in_specs = (P("tm", None, "space", None), P("tm", None, None, "space"), P(), P("tm", None))
    out_specs = (P("tm", None, None, "space", None), P("tm", None, None))
    return jax.shard_map(local, mesh=mesh, in_specs=in_specs, out_specs=out_specs, check_vma=False)
```

profile of v0, /device:TPU:0, one launch (start us, length us, event | category | flops | bytes accessed | tf_op | source)
XLA Modules:
  0.0 223.5 jit_solution(1606789766485243148)
XLA Ops:
  7.2 3.7 %copy.53 = s32[1,64,12,512]{3,2,1,0:T(8,128)} copy(s32[1,64,12,512]{3,1,2,0:T(8,128)} %param.7) | data formatting | bytes 3145728 | tf_op args[1]
  11.0 64.5 %while.17 = (s32[]{:T(128)}, f32[2,1728,64]{2,1,0:T(8,128)S(1)}, s32[64,12,512]{2,1,0:T(8,128)}, s32[27,3]{0,1:T(4,128)S(1)}, s32[]{:T(128)}, /*index=5*/bf16[12...) while((s32[]{:T(128)}, f32[2,1728,64]{2,1,0:T(8,128)S(1)}, ...), condition=%wide.region_1.2_spmd.clone, body=%wide.region_0.1_spmd.clone.sunk | while | flops 1377275648 | bytes 30928840 | solution.py:58
  11.0 0.2 fusion.44
  11.2 0.2 cosine_convert_fusion.2
  11.4 1.4 broadcast_compare_fusion.4
  12.8 6.0 %select_select_fusion.3 = (bf16[27,64,12,128]{3,2,1,0:T(8,128)(2,1)}, bf16[27,64,12,128]{3,2,1,0:T(8,128)(2,1)S(1)}) fusion(pred[64,12,128]{2,1,0:T(8,128)(4,1)S(1)} %get-tuple-element.309, pred[64,12,128]{2,1,0:T(8,128)(4,1)S(1)} %get-tuple-element.310, pred[64,12,128]{2,1,0:T(8,128)(4,1)S(1)} %get-tuple-element.311, ...), kind=kLoop, calls=%fused_computation.1.clone.1 | loop fusion | flops 15925248 | bytes 10939392 | tf_op jit(solution)/shard_map/while/body/eval_jaxpr/jit(_where)/select_n | solution.py:21
  18.8 1.0 constant_dynamic-slice_fusion.3
  19.8 4.6 %fusion.46 = f32[1728,128]{1,0:T(8,128)S(1)} fusion(bf16[1536,128]{1,0:T(8,128)(2,1)S(1)} %bitcast.66, bf16[216,8,12,128]{3,2,1,0:T(8,128)(2,1)} %bitcast.64), kind=kOutput, calls=%fused_computation.5.clone.1 | convolution fusion | flops 679477248 | bytes 6586368 | tf_op jit(solution)/shard_map/while/body/eval_jaxpr/dot_general | solution.py:51
  24.4 1.6 fusion.45
  26.0 0.5 fusion.47
  26.5 0.6 maximum_add_fusion.2
  27.2 0.2 fusion.44
  27.3 0.2 cosine_convert_fusion.2
  27.5 1.4 broadcast_compare_fusion.4
  29.0 6.0 %select_select_fusion.3 = (bf16[27,64,12,128]{3,2,1,0:T(8,128)(2,1)}, bf16[27,64,12,128]{3,2,1,0:T(8,128)(2,1)S(1)}) fusion(pred[64,12,128]{2,1,0:T(8,128)(4,1)S(1)} %get-tuple-element.309, pred[64,12,128]{2,1,0:T(8,128)(4,1)S(1)} %get-tuple-element.310, pred[64,12,128]{2,1,0:T(8,128)(4,1)S(1)} %get-tuple-element.311, ...), kind=kLoop, calls=%fused_computation.1.clone.1 | loop fusion | flops 15925248 | bytes 10939392 | tf_op jit(solution)/shard_map/while/body/eval_jaxpr/jit(_where)/select_n | solution.py:21
  34.9 1.0 constant_dynamic-slice_fusion.3
  35.9 4.6 %fusion.46 = f32[1728,128]{1,0:T(8,128)S(1)} fusion(bf16[1536,128]{1,0:T(8,128)(2,1)S(1)} %bitcast.66, bf16[216,8,12,128]{3,2,1,0:T(8,128)(2,1)} %bitcast.64), kind=kOutput, calls=%fused_computation.5.clone.1 | convolution fusion | flops 679477248 | bytes 6586368 | tf_op jit(solution)/shard_map/while/body/eval_jaxpr/dot_general | solution.py:51
  40.5 1.6 fusion.45
  42.1 0.5 fusion.47
  42.6 0.6 maximum_add_fusion.2
  43.3 0.2 fusion.44
  43.5 0.2 cosine_convert_fusion.2
  43.6 1.4 broadcast_compare_fusion.4
  45.1 6.0 %select_select_fusion.3 = (bf16[27,64,12,128]{3,2,1,0:T(8,128)(2,1)}, bf16[27,64,12,128]{3,2,1,0:T(8,128)(2,1)S(1)}) fusion(pred[64,12,128]{2,1,0:T(8,128)(4,1)S(1)} %get-tuple-element.309, pred[64,12,128]{2,1,0:T(8,128)(4,1)S(1)} %get-tuple-element.310, pred[64,12,128]{2,1,0:T(8,128)(4,1)S(1)} %get-tuple-element.311, ...), kind=kLoop, calls=%fused_computation.1.clone.1 | loop fusion | flops 15925248 | bytes 10939392 | tf_op jit(solution)/shard_map/while/body/eval_jaxpr/jit(_where)/select_n | solution.py:21
  51.0 1.0 constant_dynamic-slice_fusion.3
  52.1 4.6 %fusion.46 = f32[1728,128]{1,0:T(8,128)S(1)} fusion(bf16[1536,128]{1,0:T(8,128)(2,1)S(1)} %bitcast.66, bf16[216,8,12,128]{3,2,1,0:T(8,128)(2,1)} %bitcast.64), kind=kOutput, calls=%fused_computation.5.clone.1 | convolution fusion | flops 679477248 | bytes 6586368 | tf_op jit(solution)/shard_map/while/body/eval_jaxpr/dot_general | solution.py:51
  56.7 1.6 fusion.45
  58.2 0.5 fusion.47
  58.8 0.6 maximum_add_fusion.2
  59.4 0.2 fusion.44
  59.6 0.2 cosine_convert_fusion.2
  59.8 1.4 broadcast_compare_fusion.4
  61.2 6.0 %select_select_fusion.3 = (bf16[27,64,12,128]{3,2,1,0:T(8,128)(2,1)}, bf16[27,64,12,128]{3,2,1,0:T(8,128)(2,1)S(1)}) fusion(pred[64,12,128]{2,1,0:T(8,128)(4,1)S(1)} %get-tuple-element.309, pred[64,12,128]{2,1,0:T(8,128)(4,1)S(1)} %get-tuple-element.310, pred[64,12,128]{2,1,0:T(8,128)(4,1)S(1)} %get-tuple-element.311, ...), kind=kLoop, calls=%fused_computation.1.clone.1 | loop fusion | flops 15925248 | bytes 10939392 | tf_op jit(solution)/shard_map/while/body/eval_jaxpr/jit(_where)/select_n | solution.py:21
  67.2 1.0 constant_dynamic-slice_fusion.3
  68.2 4.6 %fusion.46 = f32[1728,128]{1,0:T(8,128)S(1)} fusion(bf16[1536,128]{1,0:T(8,128)(2,1)S(1)} %bitcast.66, bf16[216,8,12,128]{3,2,1,0:T(8,128)(2,1)} %bitcast.64), kind=kOutput, calls=%fused_computation.5.clone.1 | convolution fusion | flops 679477248 | bytes 6586368 | tf_op jit(solution)/shard_map/while/body/eval_jaxpr/dot_general | solution.py:51
  72.8 1.6 fusion.45
  74.4 0.5 fusion.47
  74.9 0.6 maximum_add_fusion.2
  75.7 2.6 %copy.26 = f32[1,2,27,64,64]{4,1,2,0,3:T(2,128)} copy(f32[1,2,27,64,64]{4,3,2,1,0:T(8,128)S(1)} %bitcast.68) | data formatting | bytes 1769472 | tf_op jit(solution)/shard_map/mul | solution.py:80
  78.3 0.6 dynamic-slice
  79.5 98.4 %all-reduce.3.cloned.1.call-done = f32[1,2,27,64,64]{4,1,2,0,3:T(2,128)} async-done(((f32[1,2,27,64,64]{4,1,2,0,3:T(2,128)}), f32[1,2,27,64,64]{4,1,2,0,3:T(2,128)}) %all-reduce.3.cloned.1.call-update) | async-done | bytes 884752
  177.9 0.9 constant_dynamic-slice_fusion.1
  178.9 5.4 %all_gather.3 = f32[2,2,27,4,64]{4,3,2,1,0:T(4,128)S(1)} all-gather(f32[1,2,27,4,64]{4,3,2,1,0:T(4,128)S(1)} %copy.32), channel_id=1, replica_groups=mesh['space'=16,'tm'=2] {'tm'}, dimensions={0}, use_global_device_ids=true | all-gather | bytes 165888 | tf_op jit(solution)/shard_map/all_gather | solution.py:82
  184.3 0.7 fusion.18
  185.0 0.7 fusion.20
  185.6 0.2 add_reduce_fusion
  186.0 30.0 %psum.7 = f32[8,2,27]{2,0,1:T(8,128)S(1)} all-reduce(f32[8,2,27]{2,0,1:T(8,128)S(1)} %pad_maximum_fusion), channel_id=1, replica_groups=mesh['space'=16,'tm'=2] {'space'}, use_global_device_ids=true, to_apply=%region_5.6 | all-reduce | flops 432 | bytes 3456 | tf_op jit(solution)/shard_map/psum | solution.py:84
  216.0 0.6 copy.33
  (30 shorter events, 0.6 us)
Async XLA Ops:
  7.2 3.8 %copy-start.1 = (s32[27,3]{0,1:T(4,128)S(1)}, s32[27,3]{0,1:T(4,128)}, u32[]{:S(2)}) copy-start(s32[27,3]{0,1:T(4,128)} %param.8) | copy-start | bytes 976
  7.2 170.8 %all-reduce.3.cloned.1.call-start = ((), (), s32[]{:S(2)}) async-start(), calls=%async_computation | async-start | bytes 3538944
  75.6 2.6 %copy-start.3 = (u32[32]{0:T(128)S(1)}, u32[32]{0:T(128)}, u32[]{:S(2)}) copy-start(u32[32]{0:T(128)} %constant.167) | copy-start | bytes 388
  75.7 3.9 %copy-start.2 = (s32[8,2]{0,1:T(2,128)S(1)}, s32[8,2]{0,1:T(2,128)}, u32[]{:S(2)}) copy-start(s32[8,2]{0,1:T(2,128)} %param.9) | copy-start | bytes 196
  178.9 7.0 %copy-start = (f32[1,2,27,4,64]{4,3,2,1,0:T(4,128)}, f32[1,2,27,4,64]{4,3,2,1,0:T(4,128)S(1)}, u32[]{:S(2)}) copy-start(f32[1,2,27,4,64]{4,3,2,1,0:T(4,128)S(1)} %copy.32) | copy-start | bytes 165892
Sparse Core Ops, SparseCore 0:
  78.4 99.5 all-reduce.2
where the time goes:
time: 224 us; the launch traced here: 223 us
  waiting for transfers between devices  98.4 us (44%)
  other arithmetic  35.8 us (16%)
  blocking collectives  35.4 us (16%)
  matrix products  25.9 us (12%)
  between operations  14.8 us (7%)
  local copies, waits for them, and re-layouts  12.7 us (6%)
    unnamed x2, waiting for transfers between devices  98.4 us
    psum x1, blocking collectives, local(): correlators = lax.psum(partial_traces, 'space') / nvec  30 us
    select_n x4, other arithmetic, phase_weights(): jnp.where(turns == 0, base_re, jnp.where(turns == 1, base_im, jnp.where(t...  23.8 us
    dot_general x4, matrix products, one_block(): left = jnp.dot(weight_re, stacked, preferred_element_type=jnp.float32)  18.3 us
    dot_general x4, matrix products, one_block(): right = jnp.dot(weight_im, stacked, preferred_element_type=jnp.float32)  6.29 us
    unnamed x13, local copies, waits for them, and re-layouts  5.89 us
    eq x4, other arithmetic, phase_weights(): turns == 0  5.79 us
    all_gather x1, blocking collectives, local(): every_slice = lax.all_gather(mesons, 'tm', axis=0, tiled=True)  5.42 us
  transfers between devices with their start and end apart: 1, of which 1 were waited for; matrix products, arithmetic and copies ran while one was open for 0% of the time, Pallas kernels for 0%

commit v1 on v0

--- a/solution.py
+++ b/solution.py
@@ -72,6 +72,10 @@
 
 
 def local(solutions, noise, momenta, pairs):
+
+    def cover_row(mine, axis_id):
+        return jnp.sum(lax.all_gather(mine, axis_id), 0)
+
     slice_count, spincol, sites_local, width = solutions.shape
     nvec = width // 2
     nspace = lax.axis_size("space")
@@ -81,7 +85,7 @@
     mesons = lax.psum_scatter(terms, "space", scatter_dimension=3, tiled=True)
     every_slice = lax.all_gather(mesons, "tm", axis=0, tiled=True)
     partial_traces = pair_traces(every_slice, pairs)
-    correlators = lax.psum(partial_traces, "space") / nvec
+    correlators = cover_row(partial_traces, "space") / nvec
     return (mesons, correlators)
 
 

time: 224 us -> 214 us (0.955)
  blocking collectives: 35.4 us -> 24.9 us
    psum x1 -> x0, blocking collectives: 30 us -> none  [local(): correlators = lax.psum(partial_traces, 'space') / nvec]
    all_gather x0 -> x1, blocking collectives: none -> 19.5 us  [cover_row(): return jnp.sum(lax.all_gather(mine, axis_id), 0)]
where the time goes in v1:
time: 214 us; the launch traced here: 213 us
  waiting for transfers between devices  98.4 us (46%)
  other arithmetic  35.9 us (17%)
  matrix products  25.9 us (12%)
  blocking collectives  24.9 us (12%)
  between operations  14.8 us (7%)
  local copies, waits for them, and re-layouts  12.7 us (6%)
    unnamed x2, waiting for transfers between devices  98.4 us
    select_n x4, other arithmetic, phase_weights(): jnp.where(turns == 0, base_re, jnp.where(turns == 1, base_im, jnp.where(t...  23.8 us
    all_gather x1, blocking collectives, cover_row(): return jnp.sum(lax.all_gather(mine, axis_id), 0)  19.5 us
    dot_general x4, matrix products, one_block(): left = jnp.dot(weight_re, stacked, preferred_element_type=jnp.float32)  18.3 us
    dot_general x4, matrix products, one_block(): right = jnp.dot(weight_im, stacked, preferred_element_type=jnp.float32)  6.29 us
    unnamed x13, local copies, waits for them, and re-layouts  5.9 us
    eq x4, other arithmetic, phase_weights(): turns == 0  5.79 us
    all_gather x1, blocking collectives, local(): every_slice = lax.all_gather(mesons, 'tm', axis=0, tiled=True)  5.42 us
  transfers between devices with their start and end apart: 1, of which 1 were waited for; matrix products, arithmetic and copies ran while one was open for 0% of the time, Pallas kernels for 0%

profile of v1, /device:TPU:0, one launch (start us, length us, event | category | flops | bytes accessed | tf_op | source)
XLA Modules:
  0.0 213.0 jit_solution(9950295105683001082)
XLA Ops:
  7.2 3.7 %copy.66 = s32[1,64,12,512]{3,2,1,0:T(8,128)} copy(s32[1,64,12,512]{3,1,2,0:T(8,128)} %param.7) | data formatting | bytes 3145728 | tf_op args[1]
  11.0 64.5 %while.17 = (s32[]{:T(128)}, f32[2,1728,64]{2,1,0:T(8,128)S(1)}, s32[64,12,512]{2,1,0:T(8,128)}, s32[27,3]{0,1:T(4,128)S(1)}, s32[]{:T(128)}, /*index=5*/bf16[12...) while((s32[]{:T(128)}, f32[2,1728,64]{2,1,0:T(8,128)S(1)}, ...), condition=%wide.region_1.2_spmd.clone, body=%wide.region_0.1_spmd.clone.sunk | while | flops 1377275648 | bytes 30928840 | solution.py:58
  11.0 0.2 fusion.44
  11.2 0.2 cosine_convert_fusion.2
  11.4 1.4 broadcast_compare_fusion.4
  12.8 6.0 %select_select_fusion.3 = (bf16[27,64,12,128]{3,2,1,0:T(8,128)(2,1)}, bf16[27,64,12,128]{3,2,1,0:T(8,128)(2,1)S(1)}) fusion(pred[64,12,128]{2,1,0:T(8,128)(4,1)S(1)} %get-tuple-element.311, pred[64,12,128]{2,1,0:T(8,128)(4,1)S(1)} %get-tuple-element.312, pred[64,12,128]{2,1,0:T(8,128)(4,1)S(1)} %get-tuple-element.313, ...), kind=kLoop, calls=%fused_computation.1.clone.1 | loop fusion | flops 15925248 | bytes 10939392 | tf_op jit(solution)/shard_map/while/body/eval_jaxpr/jit(_where)/select_n | solution.py:21
  18.8 1.0 constant_dynamic-slice_fusion.3
  19.8 4.6 %fusion.46 = f32[1728,128]{1,0:T(8,128)S(1)} fusion(bf16[1536,128]{1,0:T(8,128)(2,1)S(1)} %bitcast.69, bf16[216,8,12,128]{3,2,1,0:T(8,128)(2,1)} %bitcast.67), kind=kOutput, calls=%fused_computation.5.clone.1 | convolution fusion | flops 679477248 | bytes 6586368 | tf_op jit(solution)/shard_map/while/body/eval_jaxpr/dot_general | solution.py:51
  24.4 1.6 fusion.45
  26.0 0.5 fusion.47
  26.5 0.6 maximum_add_fusion.2
  27.2 0.2 fusion.44
  27.3 0.2 cosine_convert_fusion.2
  27.5 1.4 broadcast_compare_fusion.4
  29.0 6.0 %select_select_fusion.3 = (bf16[27,64,12,128]{3,2,1,0:T(8,128)(2,1)}, bf16[27,64,12,128]{3,2,1,0:T(8,128)(2,1)S(1)}) fusion(pred[64,12,128]{2,1,0:T(8,128)(4,1)S(1)} %get-tuple-element.311, pred[64,12,128]{2,1,0:T(8,128)(4,1)S(1)} %get-tuple-element.312, pred[64,12,128]{2,1,0:T(8,128)(4,1)S(1)} %get-tuple-element.313, ...), kind=kLoop, calls=%fused_computation.1.clone.1 | loop fusion | flops 15925248 | bytes 10939392 | tf_op jit(solution)/shard_map/while/body/eval_jaxpr/jit(_where)/select_n | solution.py:21
  34.9 1.0 constant_dynamic-slice_fusion.3
  35.9 4.6 %fusion.46 = f32[1728,128]{1,0:T(8,128)S(1)} fusion(bf16[1536,128]{1,0:T(8,128)(2,1)S(1)} %bitcast.69, bf16[216,8,12,128]{3,2,1,0:T(8,128)(2,1)} %bitcast.67), kind=kOutput, calls=%fused_computation.5.clone.1 | convolution fusion | flops 679477248 | bytes 6586368 | tf_op jit(solution)/shard_map/while/body/eval_jaxpr/dot_general | solution.py:51
  40.5 1.6 fusion.45
  42.1 0.5 fusion.47
  42.6 0.6 maximum_add_fusion.2
  43.3 0.2 fusion.44
  43.5 0.2 cosine_convert_fusion.2
  43.6 1.4 broadcast_compare_fusion.4
  45.1 6.0 %select_select_fusion.3 = (bf16[27,64,12,128]{3,2,1,0:T(8,128)(2,1)}, bf16[27,64,12,128]{3,2,1,0:T(8,128)(2,1)S(1)}) fusion(pred[64,12,128]{2,1,0:T(8,128)(4,1)S(1)} %get-tuple-element.311, pred[64,12,128]{2,1,0:T(8,128)(4,1)S(1)} %get-tuple-element.312, pred[64,12,128]{2,1,0:T(8,128)(4,1)S(1)} %get-tuple-element.313, ...), kind=kLoop, calls=%fused_computation.1.clone.1 | loop fusion | flops 15925248 | bytes 10939392 | tf_op jit(solution)/shard_map/while/body/eval_jaxpr/jit(_where)/select_n | solution.py:21
  51.0 1.0 constant_dynamic-slice_fusion.3
  52.1 4.6 %fusion.46 = f32[1728,128]{1,0:T(8,128)S(1)} fusion(bf16[1536,128]{1,0:T(8,128)(2,1)S(1)} %bitcast.69, bf16[216,8,12,128]{3,2,1,0:T(8,128)(2,1)} %bitcast.67), kind=kOutput, calls=%fused_computation.5.clone.1 | convolution fusion | flops 679477248 | bytes 6586368 | tf_op jit(solution)/shard_map/while/body/eval_jaxpr/dot_general | solution.py:51
  56.7 1.6 fusion.45
  58.2 0.5 fusion.47
  58.8 0.6 maximum_add_fusion.2
  59.4 0.2 fusion.44
  59.6 0.2 cosine_convert_fusion.2
  59.8 1.4 broadcast_compare_fusion.4
  61.2 6.0 %select_select_fusion.3 = (bf16[27,64,12,128]{3,2,1,0:T(8,128)(2,1)}, bf16[27,64,12,128]{3,2,1,0:T(8,128)(2,1)S(1)}) fusion(pred[64,12,128]{2,1,0:T(8,128)(4,1)S(1)} %get-tuple-element.311, pred[64,12,128]{2,1,0:T(8,128)(4,1)S(1)} %get-tuple-element.312, pred[64,12,128]{2,1,0:T(8,128)(4,1)S(1)} %get-tuple-element.313, ...), kind=kLoop, calls=%fused_computation.1.clone.1 | loop fusion | flops 15925248 | bytes 10939392 | tf_op jit(solution)/shard_map/while/body/eval_jaxpr/jit(_where)/select_n | solution.py:21
  67.2 1.0 constant_dynamic-slice_fusion.3
  68.2 4.6 %fusion.46 = f32[1728,128]{1,0:T(8,128)S(1)} fusion(bf16[1536,128]{1,0:T(8,128)(2,1)S(1)} %bitcast.69, bf16[216,8,12,128]{3,2,1,0:T(8,128)(2,1)} %bitcast.67), kind=kOutput, calls=%fused_computation.5.clone.1 | convolution fusion | flops 679477248 | bytes 6586368 | tf_op jit(solution)/shard_map/while/body/eval_jaxpr/dot_general | solution.py:51
  72.8 1.6 fusion.45
  74.4 0.5 fusion.47
  74.9 0.6 maximum_add_fusion.2
  75.7 2.6 %copy.37 = f32[1,2,27,64,64]{4,1,2,0,3:T(2,128)} copy(f32[1,2,27,64,64]{4,3,2,1,0:T(8,128)S(1)} %bitcast.71) | data formatting | bytes 1769472 | tf_op jit(solution)/shard_map/mul | solution.py:84
  78.3 0.6 dynamic-slice
  79.5 98.4 %all-reduce.3.cloned.1.call-done = f32[1,2,27,64,64]{4,1,2,0,3:T(2,128)} async-done(((f32[1,2,27,64,64]{4,1,2,0,3:T(2,128)}), f32[1,2,27,64,64]{4,1,2,0,3:T(2,128)}) %all-reduce.3.cloned.1.call-update) | async-done | bytes 884752
  177.9 0.9 constant_dynamic-slice_fusion.1
  178.9 5.4 %all_gather.9 = f32[2,2,27,4,64]{4,3,2,1,0:T(4,128)S(1)} all-gather(f32[1,2,27,4,64]{4,3,2,1,0:T(4,128)S(1)} %copy.43), channel_id=1, replica_groups=mesh['space'=16,'tm'=2] {'tm'}, dimensions={0}, use_global_device_ids=true | all-gather | bytes 165888 | tf_op jit(solution)/shard_map/all_gather | solution.py:86
  184.3 0.7 fusion.18
  185.0 0.7 fusion.20
  185.6 0.2 add_reduce_fusion
  186.0 19.5 %all-gather = f32[128,2,27]{2,1,0:T(2,128)S(1)} all-gather(f32[8,2,27]{2,1,0:T(2,128)S(1)} %copy.41), channel_id=2, replica_groups=mesh['space'=16,'tm'=2] {'space'}, dimensions={0}, use_global_device_ids=true | all-gather | bytes 29376 | tf_op jit(solution)/shard_map/all_gather | solution.py:77
  205.5 0.6 copy.44
  (30 shorter events, 0.6 us)
Async XLA Ops:
  7.2 3.8 %copy-start.1 = (s32[27,3]{0,1:T(4,128)S(1)}, s32[27,3]{0,1:T(4,128)}, u32[]{:S(2)}) copy-start(s32[27,3]{0,1:T(4,128)} %param.8) | copy-start | bytes 976
  7.2 170.8 %all-reduce.3.cloned.1.call-start = ((), (), s32[]{:S(2)}) async-start(), calls=%async_computation | async-start | bytes 3538944
  75.6 2.6 %copy-start.3 = (u32[32]{0:T(128)S(1)}, u32[32]{0:T(128)}, u32[]{:S(2)}) copy-start(u32[32]{0:T(128)} %constant.167) | copy-start | bytes 388
  75.7 3.9 %copy-start.2 = (s32[8,2]{0,1:T(2,128)S(1)}, s32[8,2]{0,1:T(2,128)}, u32[]{:S(2)}) copy-start(s32[8,2]{0,1:T(2,128)} %param.9) | copy-start | bytes 196
  178.9 7.0 %copy-start = (f32[1,2,27,4,64]{4,3,2,1,0:T(4,128)}, f32[1,2,27,4,64]{4,3,2,1,0:T(4,128)S(1)}, u32[]{:S(2)}) copy-start(f32[1,2,27,4,64]{4,3,2,1,0:T(4,128)S(1)} %copy.43) | copy-start | bytes 165892
Sparse Core Ops, SparseCore 0:
  78.4 99.5 all-reduce.2
